TPU v7x, 128 devices: a whole 4x4x4 slice. The times are simulated.
128 devices in a mesh: expert: 8 (over y, core), mp: 16 (over z, x).
Axes of the slice: x: 4, y: 4, z: 4, core: 2. Of those that a mesh axis runs over, the one named last changes fastest.
Arguments:
- tokens: bfloat16 [2048, 6144], P(('expert', 'mp')), may hold values from -18 to 18
- norm_gain: bfloat16 [6144], replicated, may hold values from 0.099609375 to 1.8984375
- expert_ids: int32 [2048, 2], P(('expert', 'mp')), may hold values from 0 to 7, as said below
- slot_ids: int32 [2048, 2], P(('expert', 'mp')), may hold values from 0 to 7, as said below
- route_weights: float32 [2048, 2], P(('expert', 'mp')), may hold values from 0.1 to 1
- w_gate: bfloat16 [8, 6144, 8192], P('expert', None, 'mp'), may hold values from -0.078125 to 0.078125
- w_up: bfloat16 [8, 6144, 8192], P('expert', None, 'mp'), may hold values from -0.078125 to 0.078125
- w_down: bfloat16 [8, 8192, 6144], P('expert', 'mp'), may hold values from -0.0625 to 0.0625
Outputs:
- moe_out: bfloat16 [2048, 6144], P(('expert', 'mp'))
Inputs may be any that keep to these rules, and one draw needn't show every extreme that they name: `expert_ids`: each token names two different experts. Among the 16 tokens of one device (aligned blocks of rows) no expert is named more than 8 times, and on every device some expert is named exactly 8 times. `slot_ids`: within the tokens of one device, the entries that name the same expert have different slots; slots that no entry names stay empty.
All inputs are finite; a program needn't handle non-finite values.
Results may differ from a plain program's by a relative error of at most 0.015.
Values may be sent and summed in bfloat16 or wider, within the bound.
A program may use at most 128 MiB of HBM per device.

v0:
```python
import jax
import jax.numpy as jnp
from jax import lax
from jax.sharding import PartitionSpec as P

CAP = 8


def local(tokens, norm_gain, expert_ids, slot_ids, route_weights, w_gate, w_up, w_down):
    tok_rows = tokens.shape[0]
    features = tokens.shape[1]
    experts = w_gate.shape[0] * lax.axis_size("expert")
    values = tokens.astype(jnp.float32)
    mean_square = jnp.mean(values * values, axis=1, keepdims=True)
    normed = (values * lax.rsqrt(mean_square + 1e-05) * norm_gain.astype(jnp.float32)).astype(
        jnp.bfloat16
    )
    target = expert_ids * CAP + slot_ids
    places = lax.broadcasted_iota(jnp.int32, (experts * CAP, tok_rows, 2), 0)
    placing = jnp.any(places == target[None, :, :], axis=2).astype(jnp.bfloat16)
    outgoing = jnp.dot(placing, normed, preferred_element_type=jnp.float32).astype(jnp.bfloat16)
    outgoing = outgoing.reshape(experts, CAP, features)
    gate_local = w_gate[0]
    up_local = w_up[0]
    down_local = w_down[0]
    arrived = lax.all_to_all(outgoing, "expert", split_axis=0, concat_axis=0, tiled=True)
    piece = lax.all_gather(arrived.reshape(experts * CAP, features), "mp", axis=0, tiled=True)
    gate_proj = jnp.dot(piece, gate_local, preferred_element_type=jnp.float32)
    up_proj = jnp.dot(piece, up_local, preferred_element_type=jnp.float32)
    hidden = (jax.nn.silu(gate_proj) * up_proj).astype(jnp.bfloat16)
    piece = hidden
    summed = lax.psum_scatter(
        jnp.dot(piece, down_local, preferred_element_type=jnp.float32).astype(jnp.bfloat16),
        "mp",
        scatter_dimension=0,
        tiled=True,
    )
    results = summed.reshape(experts, CAP, features)
    returned = lax.all_to_all(results, "expert", split_axis=0, concat_axis=0, tiled=True)
    flattened = returned.reshape(experts * CAP, features)
    picked = flattened[target].astype(jnp.float32)
    shares = route_weights / (route_weights[:, 0:1] + route_weights[:, 1:2])
    mixed = jnp.sum(shares[:, :, None] * picked, axis=1)
    return mixed.astype(jnp.bfloat16)


def solution(mesh):
    placed = (
        P(("expert", "mp"), None),
        P(),
        P(("expert", "mp"), None),
        P(("expert", "mp"), None),
        P(("expert", "mp"), None),
        P("expert", None, "mp"),
        P("expert", None, "mp"),
        P("expert", "mp", None),
    )
    return jax.shard_map(
        local, mesh=mesh, in_specs=placed, out_specs=P(("expert", "mp"), None), check_vma=False
    )
```

profile of v0, /device:TPU:0, one launch (start us, length us, event | category | flops | bytes accessed | tf_op | source)
XLA Modules:
  0.0 273.9 jit_solution(11265923259628819744)
XLA Ops:
  6.5 0.0 all-gather.2.cloned.1.call-start
  6.5 0.7 compare_select_fusion
  7.2 0.1 fusion.14
  7.3 0.7 convert_element_type.26
  8.0 1.1 fusion.8
  9.1 1.3 fusion
  10.5 17.7 %all_to_all.10 = bf16[8,8,6144]{2,1,0:T(8,128)(2,1)} all-to-all(bf16[8,8,6144]{2,1,0:T(8,128)(2,1)S(1)} %fusion), channel_id=1, replica_groups=mesh['expert'=8,'mp'=16] {'expert'}, dimensions={0} | all-to-all | bytes 1572864 | tf_op jit(solution)/shard_map/all_to_all | solution.py:26
  28.1 0.0 all-gather.2.cloned.1.call-update
  28.1 0.0 reduce-scatter.2.cloned.1.call-start
  28.2 90.4 %all-gather.2.cloned.1.call-done = bf16[1024,6144]{1,0:T(8,128)(2,1)} async-done(((bf16[64,6144]{1,0:T(8,128)(2,1)}), bf16[1024,6144]{1,0:T(8,128)(2,1)}) %all-gather.2.cloned.1.call-update) | async-done | bytes 12582928 | tf_op jit(solution)/shard_map/all_gather | solution.py:27
  118.6 0.0 copy-start.1
  118.6 11.6 %fusion.2 = f32[1024,512]{1,0:T(8,128)S(1)} fusion(bf16[1024,6144]{1,0:T(8,128)(2,1)} %all-gather.2.cloned.1.call-done, bf16[1,6144,512]{2,1,0:T(8,128)(2,1)} %param.14), kind=kOutput, calls=%fused_computation.5 | convolution fusion | flops 6442450944 | bytes 20971520 | tf_op jit(solution)/shard_map/dot_general | solution.py:29
  130.2 0.0 copy-done.1
  130.2 8.9 %multiply_convert_fusion = bf16[1024,512]{1,0:T(8,128)(2,1)S(1)} fusion(f32[1024,512]{1,0:T(8,128)S(1)} %fusion.2, bf16[1024,6144]{1,0:T(8,128)(2,1)S(1)} %copy-done.1, bf16[1,6144,512]{2,1,0:T(8,128)(2,1)} %param.13), kind=kOutput, calls=%fused_computation.9 | convolution fusion | flops 6445596672 | bytes 22020096 | tf_op jit(solution)/shard_map/dot_general | solution.py:28
  139.1 12.4 %convolution_convert_fusion = bf16[1024,6144]{1,0:T(8,128)(2,1)} fusion(bf16[1024,512]{1,0:T(8,128)(2,1)S(1)} %multiply_convert_fusion, bf16[1,512,6144]{2,1,0:T(8,128)(2,1)} %param.15), kind=kOutput, calls=%fused_computation.1 | convolution fusion | flops 6448742400 | bytes 19922944 | tf_op jit(solution)/shard_map/dot_general | solution.py:33
  151.5 0.0 copy-start
  151.5 0.0 reduce-scatter.2.cloned.1.call-update
  151.5 95.1 %reduce-scatter.2.cloned.1.call-done = bf16[64,6144]{1,0:T(8,128)(2,1)} async-done(((bf16[1024,6144]{1,0:T(8,128)(2,1)}), bf16[64,6144]{1,0:T(8,128)(2,1)}) %reduce-scatter.2.cloned.1.call-update) | async-done | bytes 786448 | tf_op jit(solution)/shard_map/reduce_scatter | solution.py:32
  246.6 4.3 %all-to-all-start.1 = ((bf16[8,8,6144]{2,1,0:T(8,128)(2,1)}), bf16[8,8,6144]{2,1,0:T(8,128)(2,1)S(1)}, u32[]{:S(2)}, u32[]{:S(2)}) async-start(bf16[8,8,6144]{2,1,0:T(8,128)(2,1)} %bitcast.24), calls=%async_computation.2 | async-start | bytes 1572864 | tf_op jit(solution)/shard_map/all_to_all | solution.py:39
  250.9 0.1 copy.16
  251.0 0.1 reshape.29
  251.1 0.0 copy-done
  251.1 0.1 copy.15
  251.2 12.8 %all-to-all-done.1 = bf16[8,8,6144]{2,1,0:T(8,128)(2,1)S(1)} async-done(((bf16[8,8,6144]{2,1,0:T(8,128)(2,1)}), bf16[8,8,6144]{2,1,0:T(8,128)(2,1)S(1)}, u32[]{:S(2)}, u32[]{:S(2)}) %all-to-all-start.1) | async-done | bytes 786464 | tf_op jit(solution)/shard_map/all_to_all | solution.py:39
  264.0 0.8 gather_fusion
  264.8 0.5 reshape.37
  265.3 1.7 multiply_reduce_fusion
  (4 shorter events, 0.0 us)
Async XLA Ops:
  6.5 112.0 %all-gather.2.cloned.1.call-start = ((), (), s32[]{:S(2)}) async-start(), calls=%async_computation.3 | async-start | bytes 13369344 | tf_op jit(solution)/shard_map/all_gather | solution.py:27
  28.1 218.5 %reduce-scatter.2.cloned.1.call-start = ((), (), s32[]{:S(2)}) async-start(), calls=%async_computation.4 | async-start | bytes 13369344 | tf_op jit(solution)/shard_map/reduce_scatter | solution.py:32
  118.6 11.6 %copy-start.1 = (bf16[1024,6144]{1,0:T(8,128)(2,1)S(1)}, bf16[1024,6144]{1,0:T(8,128)(2,1)}, u32[]{:S(2)}) copy-start(bf16[1024,6144]{1,0:T(8,128)(2,1)} %all-gather.2.cloned.1.call-done) | copy-start | bytes 37748740
  151.5 99.6 %copy-start = (f32[16,2]{0,1:T(2,128)S(1)}, f32[16,2]{0,1:T(2,128)}, u32[]{:S(2)}) copy-start(f32[16,2]{0,1:T(2,128)} %param.12) | copy-start | bytes 388
  246.6 17.4 %all-to-all-start.1 = ((bf16[8,8,6144]{2,1,0:T(8,128)(2,1)}), bf16[8,8,6144]{2,1,0:T(8,128)(2,1)S(1)}, u32[]{:S(2)}, u32[]{:S(2)}) async-start(bf16[8,8,6144]{2,1,0:T(8,128)(2,1)} %bitcast.24), calls=%async_computation.2 | async-start | bytes 1572864 | tf_op jit(solution)/shard_map/all_to_all | solution.py:39
Sparse Core Ops, SparseCore 0:
  28.3 90.2 all-gather.1
  151.6 94.9 reduce-scatter.1
where the time goes:
time: 275 us; the launch traced here: 274 us
  waiting for transfers between devices  198 us (72%)
  matrix products  34.2 us (12%)
  blocking collectives  17.7 us (6%)
  between operations  13.5 us (5%)
  starting transfers between devices  4.34 us (2%)
  other arithmetic  4.34 us (2%)
    reduce_scatter x1, waiting for transfers between devices, local(): lax.psum_scatter(jnp.dot(piece, down_local, preferred_element_type=jnp.fl...  95.1 us
    all_gather x1, waiting for transfers between devices, local(): lax.all_gather(arrived.reshape(experts * CAP, features), 'mp', axis=0, ti...  90.4 us
    all_to_all x1, blocking collectives, local(): lax.all_to_all(outgoing, 'expert', split_axis=0, concat_axis=0, tiled=True)  17.7 us
    all_to_all x1, waiting for transfers between devices, local(): lax.all_to_all(results, 'expert', split_axis=0, concat_axis=0, tiled=True)  12.8 us
    dot_general x1, matrix products, local(): jnp.dot(piece, down_local, preferred_element_type=jnp.float32)  12.4 us
    dot_general x1, matrix products, local(): up_proj = jnp.dot(piece, up_local, preferred_element_type=jnp.float32)  11.6 us
    dot_general x1, matrix products, local(): gate_proj = jnp.dot(piece, gate_local, preferred_element_type=jnp.float32)  8.94 us
  transfers between devices with their start and end apart: 3, of which 3 were waited for; matrix products, arithmetic and copies ran while one was open for 0% of the time, Pallas kernels for 0%

commit v1 on v0

v1 whole, which is shorter than its diff:
```python
import jax
import jax.numpy as jnp
from jax import lax
from jax.experimental import pallas as pl
from jax.experimental.pallas import tpu as pltpu
from jax.sharding import PartitionSpec as P

MESH = pl.DeviceIdType.MESH
D = 6144
PW = 2048
HW = 1024
EXT = 128
F = 512
ORDER = ((2, 1, 0), (1, 0, 2), (0, 2, 1))
REL = (0, -1, 1, 2)
RS_SUB = (2, 1, -1, 0)

RATE = 46600.0 * 0.93
LAT = 2.4
T_MM = 1.35
T_DN = 1.4
T_EV = 0.1


def plan_gather():
    t = 3.0
    free, arrive, order = {}, [], []
    done, sent = set(), set()
    weight_ready = {(0, 0): 5.0, (1, 0): 7.0, (2, 0): 9.0, (0, 1): 14.0, (1, 1): 22.0, (2, 1): 30.0}
    items = [(p, r, j) for j in (0, 1) for r in REL for p in range(3)]

    def send(p, s, k):
        ax = ORDER[p][0 if s == 0 else (1 if s < 5 else 2)]
        size = (65536 if s < 5 else 262144) // (1 if k < 2 else 2)
        if p == 2:
            size = size * 17 // 16
        way = k % 2
        begin = max(free.get((ax, way), 0.0), t)
        free[ax, way] = begin + size / RATE
        arrive.append((free[ax, way] + LAT, p, s, k))
        order.append(("send", p, s, k))

    def ready(p, s):
        got = lambda q, ks: all((p, q, k) in done for k in ks)
        if s == 0:
            return True
        if s < 5:
            return got(0, ((), (0,), (1,), (2, 3))[s - 1])
        ks = ((), (0,), (1,), (2, 3))[s - 5]
        if s == 5:
            return got(0, (0, 1, 2, 3))
        return all(got(q, ks) for q in (1, 2, 3, 4))

    def pump():
        for s in range(9):
            for p in range(3):
                if (p, s) not in sent and ready(p, s):
                    sent.add((p, s))
                    send(p, s, 0)
                    send(p, s, 1)

    def plane_ready(p, r):
        if r == 0:
            return all((p, s, k) in done for s in range(5) for k in range(4))
        ks = {-1: (0,), 1: (1,), 2: (2, 3)}[r]
        return all((p, s, k) in done for s in (5, 6, 7, 8) for k in ks)

    pump()
    while arrive or items:
        arrive.sort()
        ripe = [i for i in items if plane_ready(i[0], i[1]) and (weight_ready[i[0], i[2]] <= t or not arrive)]
        if arrive and (arrive[0][0] <= t or not ripe):
            at, p, s, k = arrive.pop(0)
            t = max(t, at) + T_EV
            done.add((p, s, k))
            order.append(("recv", p, s, k))
            if k < 2:
                send(p, s, k + 2)
            pump()
        else:
            item = ripe[0]
            items.remove(item)
            order.append(("mm",) + item)
            t += T_MM
    return order, t


def plan_scatter():
    t = 0.0
    free, arrive, order = {}, [], []
    done = set()
    items = [("dn", p, r) for r in (2, 1, -1, 0) for p in range(3)]
    todo = []
    for p in range(3):
        for st in (1, 2, 3):
            ax = ORDER[p][3 - st]
            rows = {1: 64, 2: 64, 3: 16}[st]
            size = rows * HW * 2
            for v in RS_SUB if st == 1 else (0,):
                def have(r, st=st, v=v, p=p):
                    if st == 1:
                        return ("dn", p, r)
                    if st == 2:
                        return ("own", p, 1, r)
                    return ("own", p, 2, 0)
                todo.append(((have(2),), ("rsend", p, st, v, 0, 0), ax, size))
                todo.append(((have(2),), ("rsend", p, st, v, 1, 0), ax, size))
                todo.append(((have(1),), ("rsend", p, st, v, 0, 1), ax, size))
                todo.append(((have(-1),), ("rsend", p, st, v, 1, 1), ax, size))
                todo.append(((have(1), ("rrecv", p, st, v, 0, 0)), ("rsend", p, st, v, 0, 2), ax, size))
                todo.append(((have(-1), ("rrecv", p, st, v, 1, 0)), ("rsend", p, st, v, 1, 2), ax, size))
                todo.append((
                    (have(0),) + tuple(("rrecv", p, st, v, w, q) for w in (0, 1) for q in (1, 2)),
                    ("own", p, st, v), None, 0,
                ))

    def pump():
        moved = True
        while moved:
            moved = False
            for entry in list(todo):
                needs, op, ax, size = entry
                if all(n in done for n in needs):
                    todo.remove(entry)
                    order.append(op)
                    if op[0] == "rsend":
                        _, p, st, v, way, kind = op
                        begin = max(free.get((ax, way), 0.0), t)
                        free[ax, way] = begin + size / RATE
                        arrive.append((free[ax, way] + LAT, ("rrecv", p, st, v, way, kind)))
                    else:
                        done.add(op)
                    moved = True
                    break

    while arrive or items or todo:
        arrive.sort()
        if arrive and (arrive[0][0] <= t or not items):
            at, op = arrive.pop(0)
            t = max(t, at) + T_EV
            done.add(op)
            order.append(op)
        else:
            item = items.pop(0)
            order.append(item)
            t += T_DN
            done.add(item)
        pump()
    return order, t


def kernel(
    tok, gain, ids, rw, wg, wu, wd, out, wdp,
    w0, w1, w2, g, acc, h, r1a, r1b, r2a, r2b, r3a, r3b,
    gs_sem, gr_sem, rs_sem, rr_sem, wl_sem, ws_sem, wr_sem, dl_sem,
):
    ws = (w0, w1, w2)
    ex, mp = lax.axis_index("expert"), lax.axis_index("mp")
    core, cy = lax.rem(ex, 2), lax.div(ex, 2)
    cx, cz = lax.rem(mp, 4), lax.div(mp, 4)
    me = (cz, cy, cx)
    pos = [[me[ax] if r == 0 else lax.rem(me[ax] + (r + 4) % 4, 4) for r in (0, 1, 2, -1)] for ax in range(3)]

    def at(ax, r):
        return pos[ax][r]

    def dev(ax, r):
        cc = [at(q, r if q == ax else 0) for q in range(3)]
        return (cc[1] * 2 + core, cc[0] * 4 + cc[2])

    other_core = (cy * 2 + (1 - core), mp)

    bar = pltpu.get_barrier_semaphore()
    for ax in range(3):
        for r in (1, -1):
            pl.semaphore_signal(bar, inc=1, device_id=dev(ax, r), device_id_type=MESH)
    pl.semaphore_signal(bar, inc=1, device_id=other_core, device_id_type=MESH)

    local_w = []
    for p in range(3):
        for q, src in ((0, wg), (1, wu)):
            cp = pltpu.make_async_copy(src.at[p], ws[p].at[:, :, :, :, :, pl.ds(q * F, F)], wl_sem.at[p, q])
            cp.start()
            local_w.append(cp)

    vals = tok[...].astype(jnp.float32)
    ms = jnp.mean(vals * vals, axis=1, keepdims=True)
    normed = (vals * lax.rsqrt(ms + 1e-05) * gain[...].astype(jnp.float32)).astype(jnp.bfloat16)
    g[cz, cy, cx, :, pl.ds(0, D)] = normed
    lane = lax.broadcasted_iota(jnp.int32, (16, EXT), 1)
    weights = rw[...]
    share = weights / (weights[:, 0:1] + weights[:, 1:2])
    which = ids[...]
    name = lax.rem(lane, 8)
    coef = jnp.where(name == which[:, 0:1], share[:, 0:1], 0.0) + jnp.where(name == which[:, 1:2], share[:, 1:2], 0.0)
    hi = coef.astype(jnp.bfloat16).astype(jnp.float32)
    packed = jnp.where(lane < 8, hi, jnp.where(lane < 16, coef - hi, 0.0))
    g[cz, cy, cx, :, pl.ds(D, EXT)] = packed.astype(jnp.bfloat16)

    pl.semaphore_wait(bar, 7)

    def region(p, s, r, half):
        a, b, c = ORDER[p]
        idx = [None, None, None]
        if s == 0:
            idx[a], idx[b], idx[c] = at(a, r), at(b, 0), at(c, 0)
        elif s < 5:
            idx[a], idx[b], idx[c] = at(a, REL[s - 1]), at(b, r), at(c, 0)
        else:
            idx[a], idx[b], idx[c] = slice(None), at(b, REL[s - 5]), at(c, r)
        lo, hi_ = p * PW, (p + 1) * PW + (EXT if p == 2 else 0)
        if half == 0:
            hi_ = lo + HW
        elif half == 1:
            lo = lo + HW
        return g.at[idx[0], idx[1], idx[2], :, pl.ds(lo, hi_ - lo)]

    def gcopy(p, s, k, sending):
        way = 1 if k % 2 == 0 else -1
        if sending:
            r = 0 if k < 2 else -way
        else:
            r = -way if k < 2 else 2
        reg = region(p, s, r, None if k < 2 else k - 2)
        ax = ORDER[p][0 if s == 0 else (1 if s < 5 else 2)]
        return pltpu.make_async_remote_copy(
            src_ref=reg, dst_ref=reg, send_sem=gs_sem.at[p, s, k], recv_sem=gr_sem.at[p, s, k],
            device_id=dev(ax, way), device_id_type=MESH,
        )

    def wcopy(p, q):
        src = (wg, wu)[q]
        return pltpu.make_async_remote_copy(
            src_ref=src.at[p], dst_ref=ws[p].at[:, :, :, :, :, pl.ds(2 * F + q * F, F)],
            send_sem=ws_sem.at[p, q], recv_sem=wr_sem.at[p, q], device_id=other_core, device_id_type=MESH,
        )

    dcopy = pltpu.make_async_remote_copy(
        src_ref=wd, dst_ref=wdp, send_sem=ws_sem.at[3, 0], recv_sem=wr_sem.at[3, 0],
        device_id=other_core, device_id_type=MESH,
    )

    def plane(ax, r):
        return tuple(at(ax, r) if q == ax else slice(None) for q in range(3))

    def mm(p, r, j):
        z, y, x = plane(ORDER[p][2], r)

        def tile(n, carry):
            cols = pl.ds(pl.multiple_of(j * 2 * F + n * F, F), F)
            lhs = g[z, y, x, :, pl.ds(p * PW, PW)].reshape(256, PW)
            rhs = ws[p][:, :, :, :, :, cols].reshape(PW, F)
            res = jnp.dot(lhs, rhs, preferred_element_type=jnp.float32)
            acc[z, y, x, :, cols] += res.reshape(4, 4, 16, F)
            return carry

        lax.fori_loop(0, 2, tile, 0)

    gather, _ = plan_gather()
    started = False
    have_w = set()
    acc[...] = jnp.zeros_like(acc)
    for op in gather:
        if op[0] == "send":
            gcopy(*op[1:], True).start()
        elif op[0] == "recv":
            if not started:
                started = True
                for p in range(3):
                    for q in range(2):
                        wcopy(p, q).start()
                dcopy.start()
            gcopy(*op[1:], False).wait_recv()
        else:
            _, p, r, j = op
            if (p, j) not in have_w:
                have_w.add((p, j))
                for q in range(2):
                    if j == 0:
                        local_w[p * 2 + q].wait()
                    else:
                        wcopy(p, q).wait_recv()
            mm(p, r, j)

    dcopy.wait_recv()
    down = []
    for p in range(3):
        for q, src in ((0, wd), (1, wdp)):
            cp = pltpu.make_async_copy(
                src.at[:, :, :, :, pl.ds(p * PW, PW)], ws[p].at[0, pl.ds(2 * q, 2)], dl_sem.at[p, q]
            )
            cp.start()
            down.append(cp)

    e_of = (ex, cy * 2 + (1 - core))

    def act(i, carry):
        z, y = lax.div(i, 4), lax.rem(i, 4)
        tile = g[z, y, :, :, pl.ds(D, EXT)].reshape(64, EXT).astype(jnp.float32)
        ln = lax.broadcasted_iota(jnp.int32, (64, EXT), 1)
        for j in range(2):
            mine = jnp.where((ln == e_of[j]) | (ln == e_of[j] + 8), tile, 0.0)
            cf = jnp.sum(mine, axis=1, keepdims=True)
            gate = acc[z, y, :, :, pl.ds(j * 2 * F, F)].reshape(64, F)
            up = acc[z, y, :, :, pl.ds(j * 2 * F + F, F)].reshape(64, F)
            res = gate / (1.0 + jnp.exp(-gate)) * up * cf
            h[z, y, :, :, pl.ds(j * F, F)] = res.astype(jnp.bfloat16).reshape(4, 16, F)
        return carry

    lax.fori_loop(0, 16, act, 0)

    def dn(p, r):
        z, y, x = plane(ORDER[p][2], r)

        def tile(n, carry):
            cols = pl.ds(pl.multiple_of(n * F, F), F)
            lhs = h[z, y, x].reshape(256, 2 * F)
            rhs = ws[p][0, :, :, :, :, cols].reshape(2 * F, F)
            res = jnp.dot(lhs, rhs, preferred_element_type=jnp.float32)
            ws[p][1, z, y, x, :, cols] = res.astype(jnp.bfloat16).reshape(4, 4, 16, F)
            return carry

        lax.fori_loop(0, PW // F, tile, 0)

    def part_region(p, st, v, r):
        a, b, c = ORDER[p]
        idx = [None, None, None]
        if st == 1:
            idx[a], idx[b], idx[c] = slice(None), at(b, v), at(c, r)
        elif st == 2:
            idx[a], idx[b], idx[c] = slice(None), at(b, r), at(c, 0)
        else:
            idx[a], idx[b], idx[c] = at(a, r), at(b, 0), at(c, 0)
        return tuple(idx)

    def half_cols(half):
        return pl.ds(half * HW, HW)

    def bufs(p, st, v, way):
        i = RS_SUB.index(v)
        if st == 1:
            return r1a.at[p, way, i], r1b.at[p, way, i]
        if st == 2:
            return r2a.at[p, way], r2b.at[p, way]
        return r3a.at[p, way], r3b.at[p, way]

    def slot(st, v):
        return RS_SUB.index(v) if st == 1 else st + 2

    def rcopy(p, st, v, way, kind):
        step = 1 if way == 0 else -1
        r = 2 if kind == 0 else step
        half = way if kind in (0, 2) else 1 - way
        z, y, x = part_region(p, st, v, r)
        src = ws[p].at[1, z, y, x, :, half_cols(half)]
        buf_a, buf_b = bufs(p, st, v, way)
        if kind == 0:
            dst = buf_a
        elif st == 3:
            dst = buf_b.at[:, half_cols(half)]
        else:
            dst = buf_b.at[:, :, half_cols(half)]
        return pltpu.make_async_remote_copy(
            src_ref=src, dst_ref=dst, send_sem=rs_sem.at[p, slot(st, v), way, kind],
            recv_sem=rr_sem.at[p, slot(st, v), way, kind],
            device_id=dev(ORDER[p][3 - st], step), device_id_type=MESH,
        )

    scatter, _ = plan_scatter()
    have_d = set()
    for op in scatter:
        if op[0] == "dn":
            _, p, r = op
            if p not in have_d:
                have_d.add(p)
                down[2 * p].wait()
                down[2 * p + 1].wait()
            dn(p, r)
        elif op[0] == "rsend":
            _, p, st, v, way, kind = op
            if kind == 2:
                z, y, x = part_region(p, st, v, 1 if way == 0 else -1)
                buf_a, _ = bufs(p, st, v, way)
                cols = half_cols(way)
                total = ws[p][1, z, y, x, :, cols].astype(jnp.float32) + buf_a[...].astype(jnp.float32)
                ws[p][1, z, y, x, :, cols] = total.astype(jnp.bfloat16)
            rcopy(p, st, v, way, kind).start()
        elif op[0] == "rrecv":
            rcopy(*op[1:]).wait_recv()
        else:
            _, p, st, v = op
            z, y, x = part_region(p, st, v, 0)
            b0, b1 = bufs(p, st, v, 0)[1], bufs(p, st, v, 1)[1]
            total = (
                ws[p][1, z, y, x].astype(jnp.float32) + b0[...].astype(jnp.float32) + b1[...].astype(jnp.float32)
            ).astype(jnp.bfloat16)
            if st == 3:
                out[:, pl.ds(p * PW, PW)] = total
            else:
                ws[p][1, z, y, x] = total

    for op in gather:
        if op[0] == "send":
            gcopy(*op[1:], True).wait_send()
    for op in scatter:
        if op[0] == "rsend":
            rcopy(*op[1:]).wait_send()
    for p in range(3):
        for q in range(2):
            wcopy(p, q).wait_send()
    dcopy.wait_send()


def local(tokens, norm_gain, expert_ids, slot_ids, route_weights, w_gate, w_up, w_down):
    bf = jnp.bfloat16
    vmem = pl.BlockSpec(memory_space=pltpu.VMEM)
    hbm = pl.BlockSpec(memory_space=pl.ANY)
    moe, _ = pl.pallas_call(
        kernel,
        name="moe",
        out_shape=(
            jax.ShapeDtypeStruct((16, D), bf),
            jax.ShapeDtypeStruct((2, 4, 4, 16, D), bf),
        ),
        in_specs=[vmem, vmem, vmem, vmem, hbm, hbm, hbm],
        out_specs=(vmem, hbm),
        scratch_shapes=[
            pltpu.VMEM((2, 4, 4, 4, 16, PW), bf),
            pltpu.VMEM((2, 4, 4, 4, 16, PW), bf),
            pltpu.VMEM((2, 4, 4, 4, 16, PW), bf),
            pltpu.VMEM((4, 4, 4, 16, D + EXT), bf),
            pltpu.VMEM((4, 4, 4, 16, 4 * F), jnp.float32),
            pltpu.VMEM((4, 4, 4, 16, 2 * F), bf),
            pltpu.VMEM((3, 2, 4, 4, 16, HW), bf),
            pltpu.VMEM((3, 2, 4, 4, 16, PW), bf),
            pltpu.VMEM((3, 2, 4, 16, HW), bf),
            pltpu.VMEM((3, 2, 4, 16, PW), bf),
            pltpu.VMEM((3, 2, 16, HW), bf),
            pltpu.VMEM((3, 2, 16, PW), bf),
            pltpu.SemaphoreType.DMA((3, 9, 4)),
            pltpu.SemaphoreType.DMA((3, 9, 4)),
            pltpu.SemaphoreType.DMA((3, 6, 2, 3)),
            pltpu.SemaphoreType.DMA((3, 6, 2, 3)),
            pltpu.SemaphoreType.DMA((3, 2)),
            pltpu.SemaphoreType.DMA((4, 2)),
            pltpu.SemaphoreType.DMA((4, 2)),
            pltpu.SemaphoreType.DMA((3, 2)),
        ],
        compiler_params=pltpu.CompilerParams(
            collective_id=0, has_side_effects=True, vmem_limit_bytes=67043328
        ),
    )(
        tokens,
        norm_gain.reshape(1, D),
        expert_ids,
        route_weights,
        w_gate.reshape(3, 2, 4, 4, 4, 16, F),
        w_up.reshape(3, 2, 4, 4, 4, 16, F),
        w_down.reshape(2, 4, 4, 16, D),
    )
    return moe


def solution(mesh):
    placed = (
        P(("expert", "mp"), None),
        P(),
        P(("expert", "mp"), None),
        P(("expert", "mp"), None),
        P(("expert", "mp"), None),
        P("expert", None, "mp"),
        P("expert", None, "mp"),
        P("expert", "mp", None),
    )
    return jax.shard_map(
        local, mesh=mesh, in_specs=placed, out_specs=P(("expert", "mp"), None), check_vma=False
    )
```

time: 275 us -> 142 us (0.52)
  waiting for transfers between devices: 198 us -> 0 us
  Pallas kernels: 0 us -> 137 us
  matrix products: 34.2 us -> 0 us
  blocking collectives: 17.7 us -> 0 us
  between operations: 13.5 us -> 0.01 us
  other arithmetic: 4.34 us -> 0 us
  starting transfers between devices: 4.34 us -> 0 us
  local copies, waits for them, and re-layouts: 1.54 us -> 5.64 us
    pallas_call x0 -> x1, Pallas kernels: none -> 137 us  [local(): pl.pallas_call(kernel, name='moe', out_shape=(jax.ShapeDtypeStruct((16, D...]
    reduce_scatter x1 -> x0, waiting for transfers between devices: 95.1 us -> none  [local(): lax.psum_scatter(jnp.dot(piece, down_local, preferred_element_type=jnp.fl...]
    all_gather x1 -> x0, waiting for transfers between devices: 90.4 us -> none  [local(): lax.all_gather(arrived.reshape(experts * CAP, features), 'mp', axis=0, ti...]
    dot_general x4 -> x0, matrix products: 34.2 us -> none  [the longest x1 12.4 us: local(): jnp.dot(piece, down_local, preferred_element_type=jnp.float32)]
    all_to_all x1 -> x0, blocking collectives: 17.7 us -> none  [local(): lax.all_to_all(outgoing, 'expert', split_axis=0, concat_axis=0, tiled=True)]
    all_to_all x1 -> x0, waiting for transfers between devices: 12.8 us -> none  [local(): lax.all_to_all(results, 'expert', split_axis=0, concat_axis=0, tiled=True)]
    unnamed x4 -> x3, local copies, waits for them, and re-layouts: 0.01 us -> 4.32 us
    all_to_all x1 -> x0, starting transfers between devices: 4.29 us -> none  [local(): lax.all_to_all(results, 'expert', split_axis=0, concat_axis=0, tiled=True)]
  transfers between devices with their start and end apart: 3 -> 0, of which waited for: 3 -> 0; matrix products, arithmetic and copies ran while one was open for 0% -> 0% of each run, Pallas kernels for 0% -> 0%
where the time goes in v1:
time: 142 us
  Pallas kernels  137 us (96%)
  local copies, waits for them, and re-layouts  5.64 us (4%)
    pallas_call x1, Pallas kernels, local(): pl.pallas_call(kernel, name='moe', out_shape=(jax.ShapeDtypeStruct((16, D...  137 us
    unnamed x3, local copies, waits for them, and re-layouts  4.32 us

profile of v1, /device:TPU:0, one launch (start us, length us, event | category | flops | bytes accessed | tf_op | source)
XLA Modules:
  0.0 142.2 jit_solution(3155446273492733435)
XLA Ops:
  0.0 1.4 copy.8.ids
  1.4 1.3 copy.9.rw
  2.7 1.3 reshape.12.gain
  4.0 136.6 %moe.1 = (bf16[16,6144]{1,0:T(8,128)(2,1)}, bf16[2,4,4,16,6144]{4,3,2,1,0:T(8,128)(2,1)}) custom-call(bf16[16,6144]{1,0:T(8,128)(2,1)} %tok.1, bf16[1,6144]{1,0:T(2,128)(2,1)} %reshape.12.gain, s32[16,2]{1,0:T(8,128)} %copy.8.ids, f32[16,2]{1,0:T(8,128)} %copy.9.rw, bf16[3,2,4,4,4,16,512]{6,5,4,3,2,1,0:T(8,128)(2,1)} %bitcast.3, ...), custom_call_target="tpu_custom_call" | custom-call | tf_op jit(solution)/shard_map/moe/pallas_call | solution.py:418
  140.6 1.6 %copy.11 = bf16[16,6144]{1,0:T(8,128)(2,1)} copy(bf16[16,6144]{1,0:T(8,128)(2,1)} %get-tuple-element.6) | data formatting | bytes 393216

commit v2 on v1

--- a/solution.py
+++ b/solution.py
@@ -15,61 +15,78 @@
 REL = (0, -1, 1, 2)
 RS_SUB = (2, 1, -1, 0)
 
-RATE = 46600.0 * 0.93
-LAT = 2.4
-T_MM = 1.35
-T_DN = 1.4
-T_EV = 0.1
+RATE = 46600.0 * 0.98
+LAT = 2.0
+T_MM = 1.15
+T_DN = 1.1
+T_EV = 0.06
+WEIGHT = ((5.0, 6.0, 7.0), (14.0, 20.0, 26.0))
+
+
+def axis_of(s):
+    return 0 if s == 0 else (1 if s < 5 else 2)
 
 
 def plan_gather():
-    t = 3.0
+    t = 2.0
     free, arrive, order = {}, [], []
-    done, sent = set(), set()
-    weight_ready = {(0, 0): 5.0, (1, 0): 7.0, (2, 0): 9.0, (0, 1): 14.0, (1, 1): 22.0, (2, 1): 30.0}
-    items = [(p, r, j) for j in (0, 1) for r in REL for p in range(3)]
-
-    def send(p, s, k):
-        ax = ORDER[p][0 if s == 0 else (1 if s < 5 else 2)]
-        size = (65536 if s < 5 else 262144) // (1 if k < 2 else 2)
+    done, sent, held = set(), set(), {}
+    weight_ready = {(p, j): WEIGHT[j][p] for p in range(3) for j in range(2)}
+    passes = [(p, n, j) for n in range(4) for j in (0, 1) for p in range(3)]
+
+    def put(p, s, k):
+        size = (65536 if s < 9 else 262144) // (1 if k < 2 else 2)
         if p == 2:
             size = size * 17 // 16
-        way = k % 2
-        begin = max(free.get((ax, way), 0.0), t)
-        free[ax, way] = begin + size / RATE
-        arrive.append((free[ax, way] + LAT, p, s, k))
+        link = (ORDER[p][axis_of(s)], k % 2)
+        begin = max(free.get(link, 0.0), t)
+        free[link] = begin + size / RATE
+        arrive.append((free[link] + LAT, p, s, k))
         order.append(("send", p, s, k))
+
+    def send(p, s, k):
+        if k > 1 and s >= 5 and not all((p, q) in sent for q in range(5, 12)):
+            held.setdefault(p, []).append((p, s, k))
+        else:
+            put(p, s, k)
 
     def ready(p, s):
         got = lambda q, ks: all((p, q, k) in done for k in ks)
         if s == 0:
             return True
-        if s < 5:
-            return got(0, ((), (0,), (1,), (2, 3))[s - 1])
-        ks = ((), (0,), (1,), (2, 3))[s - 5]
-        if s == 5:
-            return got(0, (0, 1, 2, 3))
-        return all(got(q, ks) for q in (1, 2, 3, 4))
+        if s < 9:
+            return got(0, ((), (0,), (1,), (2, 3))[(s - 1) % 4])
+        return all(got(q, ((0,), (1,), (2, 3))[s - 9]) for q in (1, 2, 3, 4))
 
     def pump():
-        for s in range(9):
+        for s in range(12):
             for p in range(3):
                 if (p, s) not in sent and ready(p, s):
                     sent.add((p, s))
                     send(p, s, 0)
                     send(p, s, 1)
-
-    def plane_ready(p, r):
-        if r == 0:
-            return all((p, s, k) in done for s in range(5) for k in range(4))
-        ks = {-1: (0,), 1: (1,), 2: (2, 3)}[r]
-        return all((p, s, k) in done for s in (5, 6, 7, 8) for k in ks)
+        for p in range(3):
+            if p in held and all((p, q) in sent for q in range(5, 12)):
+                for entry in held.pop(p):
+                    put(*entry)
+
+    def ripe(p, n, j):
+        if n == 0:
+            ok = all((p, s, k) in done for s in range(5) for k in range(4))
+        elif n == 1:
+            ok = all((p, s, k) in done for s in range(5, 10) for k in range(2))
+        elif n == 2:
+            ok = all((p, s, k) in done for s in (10, 11) for k in range(2))
+        else:
+            ok = all((p, s, k) in done for s in range(5, 12) for k in (2, 3))
+        return ok and (weight_ready[p, j] <= t or not arrive)
 
     pump()
-    while arrive or items:
+    last = None
+    while arrive or passes:
         arrive.sort()
-        ripe = [i for i in items if plane_ready(i[0], i[1]) and (weight_ready[i[0], i[2]] <= t or not arrive)]
-        if arrive and (arrive[0][0] <= t or not ripe):
+        now = [i for i in passes if ripe(*i)]
+        if arrive and (arrive[0][0] <= t or not now):
             at, p, s, k = arrive.pop(0)
             t = max(t, at) + T_EV
             done.add((p, s, k))
@@ -77,12 +94,18 @@
             if k < 2:
                 send(p, s, k + 2)
             pump()
-        else:
-            item = ripe[0]
-            items.remove(item)
+            if not arrive:
+                last = t
+        else:
+            if not arrive:
+                now.sort(key=lambda i: (i[0], i[1], i[2]))
+            item = now[0]
+            passes.remove(item)
             order.append(("mm",) + item)
+            if not any(i[0] == item[0] for i in passes):
+                order.append(("wd", item[0]))
             t += T_MM
-    return order, t
+    return order, t, last
 
 
 def plan_scatter():
@@ -185,14 +208,23 @@
 
     vals = tok[...].astype(jnp.float32)
     ms = jnp.mean(vals * vals, axis=1, keepdims=True)
-    normed = (vals * lax.rsqrt(ms + 1e-05) * gain[...].astype(jnp.float32)).astype(jnp.bfloat16)
-    g[cz, cy, cx, :, pl.ds(0, D)] = normed
+    inv = lax.rsqrt(ms + 1e-05)
+    scale = gain[...].astype(jnp.float32)
+    for i in range(D // 128):
+        piece = vals[:, i * 128:(i + 1) * 128] * inv * scale[i:i + 1, :]
+        g[cz, cy, cx, :, pl.ds(i * 128, 128)] = piece.astype(jnp.bfloat16)
     lane = lax.broadcasted_iota(jnp.int32, (16, EXT), 1)
+    diag = lax.broadcasted_iota(jnp.int32, (16, 16), 0) == lax.broadcasted_iota(jnp.int32, (16, 16), 1)
+
+    def column(row):
+        return jnp.sum(jnp.where(diag, row, 0.0), axis=1, keepdims=True)
+
     weights = rw[...]
-    share = weights / (weights[:, 0:1] + weights[:, 1:2])
-    which = ids[...]
-    name = lax.rem(lane, 8)
-    coef = jnp.where(name == which[:, 0:1], share[:, 0:1], 0.0) + jnp.where(name == which[:, 1:2], share[:, 1:2], 0.0)
+    share = weights / (weights[0:1, :] + weights[1:2, :])
+    which = ids[...].astype(jnp.float32)
+    name = lax.rem(lane, 8).astype(jnp.float32)
+    coef = jnp.where(name == column(which[0:1, :]), column(share[0:1, :]), 0.0)
+    coef = coef + jnp.where(name == column(which[1:2, :]), column(share[1:2, :]), 0.0)
     hi = coef.astype(jnp.bfloat16).astype(jnp.float32)
     packed = jnp.where(lane < 8, hi, jnp.where(lane < 16, coef - hi, 0.0))
     g[cz, cy, cx, :, pl.ds(D, EXT)] = packed.astype(jnp.bfloat16)
@@ -206,8 +238,10 @@
             idx[a], idx[b], idx[c] = at(a, r), at(b, 0), at(c, 0)
         elif s < 5:
             idx[a], idx[b], idx[c] = at(a, REL[s - 1]), at(b, r), at(c, 0)
-        else:
-            idx[a], idx[b], idx[c] = slice(None), at(b, REL[s - 5]), at(c, r)
+        elif s < 9:
+            idx[a], idx[b], idx[c] = at(a, REL[s - 5]), at(b, 0), at(c, r)
+        else:
+            idx[a], idx[b], idx[c] = slice(None), at(b, REL[s - 8]), at(c, r)
         lo, hi_ = p * PW, (p + 1) * PW + (EXT if p == 2 else 0)
         if half == 0:
             hi_ = lo + HW
@@ -222,7 +256,7 @@
         else:
             r = -way if k < 2 else 2
         reg = region(p, s, r, None if k < 2 else k - 2)
-        ax = ORDER[p][0 if s == 0 else (1 if s < 5 else 2)]
+        ax = ORDER[p][axis_of(s)]
         return pltpu.make_async_remote_copy(
             src_ref=reg, dst_ref=reg, send_sem=gs_sem.at[p, s, k], recv_sem=gr_sem.at[p, s, k],
             device_id=dev(ax, way), device_id_type=MESH,
@@ -243,23 +277,34 @@
     def plane(ax, r):
         return tuple(at(ax, r) if q == ax else slice(None) for q in range(3))
 
-    def mm(p, r, j):
-        z, y, x = plane(ORDER[p][2], r)
-
-        def tile(n, carry):
-            cols = pl.ds(pl.multiple_of(j * 2 * F + n * F, F), F)
+    def mm(p, n, j):
+        cols = pl.ds(j * 2 * F, 2 * F)
+        rhs = ws[p][:, :, :, :, :, cols].reshape(PW, 2 * F)
+        if n in (0, 3):
+            z, y, x = plane(ORDER[p][2], 0 if n == 0 else 2)
             lhs = g[z, y, x, :, pl.ds(p * PW, PW)].reshape(256, PW)
-            rhs = ws[p][:, :, :, :, :, cols].reshape(PW, F)
             res = jnp.dot(lhs, rhs, preferred_element_type=jnp.float32)
-            acc[z, y, x, :, cols] += res.reshape(4, 4, 16, F)
-            return carry
-
-        lax.fori_loop(0, 2, tile, 0)
-
-    gather, _ = plan_gather()
+            acc[z, y, x, :, cols] += res.reshape(4, 4, 16, 2 * F)
+            return
+        pieces = []
+        for v in REL[2 * n - 2:2 * n]:
+            for r in (-1, 1):
+                idx = [slice(None)] * 3
+                idx[ORDER[p][1]], idx[ORDER[p][2]] = at(ORDER[p][1], v), at(ORDER[p][2], r)
+                pieces.append(tuple(idx))
+        lhs = jnp.concatenate([g[z, y, x, :, pl.ds(p * PW, PW)].reshape(64, PW) for z, y, x in pieces], axis=0)
+        res = jnp.dot(lhs, rhs, preferred_element_type=jnp.float32)
+        for i, (z, y, x) in enumerate(pieces):
+            acc[z, y, x, :, cols] += res[64 * i:64 * i + 64].reshape(4, 16, 2 * F)
+
+    def down(p, q):
+        return pltpu.make_async_copy(
+            (wd, wdp)[q].at[:, :, :, :, pl.ds(p * PW, PW)], ws[p].at[0, pl.ds(2 * q, 2)], dl_sem.at[p, q]
+        )
+
+    gather = plan_gather()[0]
     started = False
     have_w = set()
-    acc[...] = jnp.zeros_like(acc)
     for op in gather:
         if op[0] == "send":
             gcopy(*op[1:], True).start()
@@ -270,9 +315,15 @@
                     for q in range(2):
                         wcopy(p, q).start()
                 dcopy.start()
+                acc[...] = jnp.zeros_like(acc)
             gcopy(*op[1:], False).wait_recv()
-        else:
-            _, p, r, j = op
+        elif op[0] == "wd":
+            if op[1] == 0:
+                dcopy.wait_recv()
+            for q in range(2):
+                down(op[1], q).start()
+        else:
+            _, p, n, j = op
             if (p, j) not in have_w:
                 have_w.add((p, j))
                 for q in range(2):
@@ -280,22 +331,12 @@
                         local_w[p * 2 + q].wait()
                     else:
                         wcopy(p, q).wait_recv()
-            mm(p, r, j)
-
-    dcopy.wait_recv()
-    down = []
-    for p in range(3):
-        for q, src in ((0, wd), (1, wdp)):
-            cp = pltpu.make_async_copy(
-                src.at[:, :, :, :, pl.ds(p * PW, PW)], ws[p].at[0, pl.ds(2 * q, 2)], dl_sem.at[p, q]
-            )
-            cp.start()
-            down.append(cp)
+            mm(p, n, j)
 
     e_of = (ex, cy * 2 + (1 - core))
 
     def act(i, carry):
-        z, y = lax.div(i, 4), lax.rem(i, 4)
+        z, y = lax.rem(cz + lax.div(i, 4), 4), lax.rem(i, 4)
         tile = g[z, y, :, :, pl.ds(D, EXT)].reshape(64, EXT).astype(jnp.float32)
         ln = lax.broadcasted_iota(jnp.int32, (64, EXT), 1)
         for j in range(2):
@@ -307,20 +348,18 @@
             h[z, y, :, :, pl.ds(j * F, F)] = res.astype(jnp.bfloat16).reshape(4, 16, F)
         return carry
 
-    lax.fori_loop(0, 16, act, 0)
-
     def dn(p, r):
         z, y, x = plane(ORDER[p][2], r)
 
         def tile(n, carry):
-            cols = pl.ds(pl.multiple_of(n * F, F), F)
+            cols = pl.ds(pl.multiple_of(n * HW, HW), HW)
             lhs = h[z, y, x].reshape(256, 2 * F)
-            rhs = ws[p][0, :, :, :, :, cols].reshape(2 * F, F)
+            rhs = ws[p][0, :, :, :, :, cols].reshape(2 * F, HW)
             res = jnp.dot(lhs, rhs, preferred_element_type=jnp.float32)
-            ws[p][1, z, y, x, :, cols] = res.astype(jnp.bfloat16).reshape(4, 4, 16, F)
+            ws[p][1, z, y, x, :, cols] = res.astype(jnp.bfloat16).reshape(4, 4, 16, HW)
             return carry
 
-        lax.fori_loop(0, PW // F, tile, 0)
+        lax.fori_loop(0, 2, tile, 0)
 
     def part_region(p, st, v, r):
         a, b, c = ORDER[p]
@@ -366,15 +405,20 @@
             device_id=dev(ORDER[p][3 - st], step), device_id_type=MESH,
         )
 
-    scatter, _ = plan_scatter()
+    scatter = plan_scatter()[0]
     have_d = set()
     for op in scatter:
         if op[0] == "dn":
             _, p, r = op
             if p not in have_d:
                 have_d.add(p)
-                down[2 * p].wait()
-                down[2 * p + 1].wait()
+                if p == 0:
+                    lax.fori_loop(8, 12, act, 0)
+                elif p == 1:
+                    lax.fori_loop(0, 8, act, 0)
+                    lax.fori_loop(12, 16, act, 0)
+                down(p, 0).wait()
+                down(p, 1).wait()
             dn(p, r)
         elif op[0] == "rsend":
             _, p, st, v, way, kind = op
@@ -437,8 +481,8 @@
             pltpu.VMEM((3, 2, 4, 16, PW), bf),
             pltpu.VMEM((3, 2, 16, HW), bf),
             pltpu.VMEM((3, 2, 16, PW), bf),
-            pltpu.SemaphoreType.DMA((3, 9, 4)),
-            pltpu.SemaphoreType.DMA((3, 9, 4)),
+            pltpu.SemaphoreType.DMA((3, 12, 4)),
+            pltpu.SemaphoreType.DMA((3, 12, 4)),
             pltpu.SemaphoreType.DMA((3, 6, 2, 3)),
             pltpu.SemaphoreType.DMA((3, 6, 2, 3)),
             pltpu.SemaphoreType.DMA((3, 2)),
@@ -451,9 +495,9 @@
         ),
     )(
         tokens,
-        norm_gain.reshape(1, D),
-        expert_ids,
-        route_weights,
+        norm_gain.reshape(D // 128, 128),
+        expert_ids.T,
+        route_weights.T,
         w_gate.reshape(3, 2, 4, 4, 4, 16, F),
         w_up.reshape(3, 2, 4, 4, 4, 16, F),
         w_down.reshape(2, 4, 4, 16, D),

time: 142 us -> 126 us (0.89)
  Pallas kernels: 137 us -> 124 us
  local copies, waits for them, and re-layouts: 5.64 us -> 1.62 us
    pallas_call x1, Pallas kernels: 137 us -> 124 us  [local(): pl.pallas_call(kernel, name='moe', out_shape=(jax.ShapeDtypeStruct((16, D...]
    unnamed x3 -> x1, local copies, waits for them, and re-layouts: 4.32 us -> 1.62 us
where the time goes in v2:
time: 126 us
  Pallas kernels  124 us (98%)
  local copies, waits for them, and re-layouts  1.62 us (1%)
    pallas_call x1, Pallas kernels, local(): pl.pallas_call(kernel, name='moe', out_shape=(jax.ShapeDtypeStruct((16, D...  124 us

profile of v2, /device:TPU:0, one launch (start us, length us, event | category | flops | bytes accessed | tf_op | source)
XLA Modules:
  0.0 125.8 jit_solution(18276316435081542747)
XLA Ops:
  0.0 124.2 %moe.1 = (bf16[16,6144]{1,0:T(8,128)(2,1)}, bf16[2,4,4,16,6144]{4,3,2,1,0:T(8,128)(2,1)}) custom-call(bf16[16,6144]{1,0:T(8,128)(2,1)} %tok.1, bf16[48,128]{1,0:T(8,128)(2,1)} %bitcast.9, s32[2,16]{1,0:T(2,128)} %bitcast.10, f32[2,16]{1,0:T(2,128)} %bitcast.11, bf16[3,2,4,4,4,16,512]{6,5,4,3,2,1,0:T(8,128)(2,1)} %bitcast.6, ...), custom_call_target="tpu_custom_call" | custom-call | tf_op jit(solution)/shard_map/moe/pallas_call | solution.py:462
  124.2 1.6 %copy.9 = bf16[16,6144]{1,0:T(8,128)(2,1)} copy(bf16[16,6144]{1,0:T(8,128)(2,1)} %get-tuple-element.6) | data formatting | bytes 393216
